TPU v7x, 256 devices: a whole 4x4x8 slice. The times are simulated.
256 devices in a mesh: rep: 16 (over x, z_hi, core), stripe: 16 (over y, z_lo).
Axes of the slice: x: 4, y: 4, z: 8 (z_hi: 2, z_lo: 4; z = z_hi * 4 + z_lo), core: 2. Of those that a mesh axis runs over, the one named last changes fastest.
Arguments:
- activations: bfloat16 [4096, 4096], P('rep'), may hold values from -6 to 6
- out_grads: bfloat16 [4096, 8192], P('rep', 'stripe'), may hold values from -4 to 4
- statistics: float32 [16, 16, 512, 512], P('rep', 'stripe'), may hold values from -48 to 4608, as said below
- owner_blocks: int32 [16, 8], P('stripe'), may hold values from 0 to 7, each once within a row
Outputs:
- preconditioned: float32 [4096, 8192], P(None, 'stripe')
- new_stats: float32 [16, 16, 512, 512], P('rep', 'stripe')
Inputs may be any that keep to these rules, and one draw needn't show every extreme that they name: statistics[p, s] is symmetric positive definite for every p and s. `owner_blocks`: each row lists every row block 0 to 7 exactly once.
All inputs are finite; a program needn't handle non-finite values.
Results may differ from a plain program's by a relative error of at most 0.0003.
Values sent between devices are 32-bit elements; how exact they have to be, the bound alone decides.
A program may use at most 128 MiB of HBM per device.

v0:
```python
import jax
import jax.numpy as jnp
from jax import lax
from jax.sharding import Mesh
from jax.sharding import PartitionSpec as P

BLOCK = 512
ITERS = 2
REP = ("rep_0", "rep_1", "rep_2")
REP_STRIPE = ("rep_0", "rep_1", "rep_2", "stripe_0", "stripe_1")
STRIPE = ("stripe_0", "stripe_1")
decay_rate = 0.95
damping = 0.25
epsilon = 1e-06
highest = lax.Precision.HIGHEST


def partner(shard, axis, stride):
    return lax.ppermute(shard, axis, [(i, i ^ 1 << stride) for i in range(lax.axis_size(axis))])


def by_axis(shard, axes):
    for axis in axes:
        shard = lax.psum(shard, axis)
    return shard


def inverse_root(damped):
    identity = jnp.eye(damped.shape[-1], dtype=damped.dtype)
    frob_norm = jnp.sqrt(jnp.sum(damped * damped, axis=(-2, -1), keepdims=True) + epsilon)
    scaled = damped / frob_norm
    root_now = identity * frob_norm ** (-0.25)
    for sweep in range(ITERS):
        factor = (5.0 * identity - scaled) * 0.25
        root_now = jnp.matmul(root_now, factor, precision=highest)
        if sweep + 1 < ITERS:
            square = jnp.matmul(factor, factor, precision=highest)
            fourth = jnp.matmul(square, square, precision=highest)
            scaled = jnp.matmul(fourth, scaled, precision=highest)
    return root_now


def slot_terms(activations, out_grads, blocks_of, pair_count, piece_rows, row_count):
    tokens_here, in_width = activations.shape
    per_block = BLOCK // piece_rows
    shaped = activations.reshape(tokens_here, in_width // piece_rows, piece_rows)
    slot_count = row_count // piece_rows
    slot_ids = jnp.arange(slot_count, dtype=jnp.int32)
    block_ids = jnp.take(blocks_of, slot_ids % pair_count)
    half_ids = slot_ids // pair_count % per_block
    chosen = jnp.take(shaped, block_ids * per_block + half_ids, axis=1)
    products = jnp.einsum("tkp,tc->kpc", chosen, out_grads, preferred_element_type=jnp.float32)
    return products.reshape(slot_count * piece_rows, out_grads.shape[1])


def per_device(activations, out_grads, statistics, owner_blocks):
    rep_count = lax.axis_size(REP)
    pair_count = rep_count // 2
    pair_bit = rep_count.bit_length() - 2
    half_rows = BLOCK // 2
    my_index = lax.axis_index(REP)
    is_left = my_index < pair_count
    blocks_of = owner_blocks[0]
    own_half = lax.psum_scatter(
        slot_terms(
            activations, out_grads, blocks_of, pair_count, half_rows, half_rows * lax.axis_size(REP)
        ),
        REP,
        scatter_dimension=0,
        tiled=True,
    )
    partner_half = partner(own_half, REP, pair_bit)
    gradient = jnp.where(
        is_left,
        jnp.concatenate([own_half, partner_half], axis=0),
        jnp.concatenate([partner_half, own_half], axis=0),
    )
    facing = jnp.where(is_left, gradient, gradient.T)
    new_stat = decay_rate * statistics[0, 0] + jnp.dot(facing, facing.T, precision=highest)
    trace_sum = by_axis(jnp.trace(new_stat), REP_STRIPE)
    mean_diag = trace_sum / (rep_count * lax.axis_size(STRIPE) * BLOCK)
    identity = jnp.eye(BLOCK, dtype=jnp.float32)
    root_now = inverse_root(new_stat + damping * mean_diag * identity)
    partner_root = partner(root_now, REP, pair_bit)
    left_root = jnp.where(is_left, root_now, partner_root)
    right_root = jnp.where(is_left, partner_root, root_now)
    row_start = jnp.where(is_left, 0, half_rows).astype(jnp.int32)
    my_rows = lax.dynamic_slice_in_dim(left_root, row_start, half_rows, 0)
    grad_rows = lax.dynamic_slice_in_dim(gradient, row_start, half_rows, 0)
    precond_half = jnp.dot(
        jnp.dot(my_rows, gradient, precision=highest), right_root, precision=highest
    )
    grad_sq, prec_sq = (
        by_axis(jnp.sum(grad_rows * grad_rows), REP_STRIPE),
        by_axis(jnp.sum(precond_half * precond_half), REP_STRIPE),
    )
    scaled = precond_half * jnp.sqrt(grad_sq / (prec_sq + epsilon))
    gathered = lax.all_gather(scaled[None], REP, axis=0, tiled=True)
    pair_ids = jnp.arange(pair_count, dtype=jnp.int32)
    inverse = jnp.sum(
        pair_ids[:, None] * (blocks_of[:, None] == pair_ids[None, :]).astype(jnp.int32), axis=0
    )
    row_order = jnp.stack([inverse, inverse + pair_count], axis=1).reshape(-1)
    preconditioned = jnp.take(gathered, row_order, axis=0).reshape(
        pair_count * BLOCK, gathered.shape[2]
    )
    return (preconditioned, new_stat[None, None])


def solution(mesh):
    split = Mesh(
        mesh.devices.reshape(4, 2, 2, 4, 4), ("rep_0", "rep_1", "rep_2", "stripe_0", "stripe_1")
    )
    return jax.shard_map(
        per_device,
        mesh=split,
        in_specs=(P(REP, None), P(REP, STRIPE), P(REP, STRIPE, None, None), P(STRIPE, None)),
        out_specs=(P(None, STRIPE), P(REP, STRIPE, None, None)),
        check_vma=False,
    )
```

profile of v0, /device:TPU:1, one launch (start us, length us, event | category | flops | bytes accessed | tf_op | source)
XLA Modules:
  0.0 449.1 jit_solution(16025409931431591571)
XLA Ops:
  8.2 1.3 gather_fusion
  9.6 4.1 copy.26
  13.7 2.8 copy.27
  16.5 2.0 gather_fusion.1
  18.5 6.7 %fusion = f32[16,256,512]{2,1,0:T(8,128)} fusion(bf16[16,256,256]{2,1,0:T(8,128)(2,1)} %gather_fusion.1, pred[16]{0:T(512)(128)(4,1)S(1)} %get-tuple-element.16, bf16[256,512]{1,0:T(8,128)(2,1)S(1)} %copy-done), kind=kOutput, calls=%fused_computation.4 | convolution fusion | flops 1074790400 | bytes 10747920 | tf_op jit(solution)/shard_map/tkp,tc->kpc/dot_general | solution.py:52
  25.2 8.9 %copy.29 = f32[4096,512]{0,1:T(8,128)} copy(f32[4096,512]{1,0:T(8,128)} %bitcast.40) | data formatting | bytes 16777216 | tf_op jit(solution)/shard_map/reshape | solution.py:53
  34.2 142.1 %reduce-scatter.2.cloned.1.call-done = f32[256,512]{0,1:T(8,128)} async-done(((f32[4096,512]{0,1:T(8,128)}), f32[256,512]{0,1:T(8,128)}) %reduce-scatter.2.cloned.1.call-update) | async-done | bytes 524304 | tf_op jit(solution)/shard_map/reduce_scatter | solution.py:64
  176.3 1.2 collective-permute-start
  177.5 11.7 %collective-permute-done = f32[256,512]{0,1:T(8,128)S(1)} collective-permute-done((f32[256,512]{0,1:T(8,128)}, f32[256,512]{0,1:T(8,128)S(1)}, u32[]{:S(2)}, u32[]{:S(2)}) %collective-permute-start) | collective-permute-done | bytes 524320 | tf_op jit(solution)/shard_map/ppermute | solution.py:19
  189.3 1.6 maximum_select_fusion
  191.2 5.6 %select_reduce_fusion = (f32[]{:T(128)}, f32[512,512]{1,0:T(8,128)S(1)}) fusion(f32[512,512]{1,0:T(8,128)S(1)} %copy.31, pred[]{:T(512)S(6)} %lt.75, f32[256,512]{0,1:T(8,128)} %reduce-scatter.2.cloned.1.call-done, f32[256,512]{0,1:T(8,128)} %copy-done.3, f32[1,1,512,512]{3,2,1,0:T(8,128)} %param.6), kind=kOutput, calls=%fused_computation.22 | convolution fusion | flops 1612972032 | bytes 4194309 | tf_op jit(solution)/shard_map/dot_general | solution.py:79
  196.8 6.6 %psum.105 = f32[]{:T(128)} all-reduce(f32[]{:T(128)} %get-tuple-element.12), channel_id=1, replica_groups=mesh['rep_0'=4,'rep_1'=2,'rep_2'=2,'stripe_0'=4,'stripe_1'=4] {'rep_0'}, use_global_device_ids=true, to_apply=%region_3.4 | all-reduce | flops 1 | bytes 8 | tf_op jit(solution)/shard_map/psum | solution.py:24
  203.4 8.3 %psum.106 = f32[]{:T(128)} all-reduce(f32[]{:T(128)} %psum.105), channel_id=1, replica_groups=mesh['rep_0'=4,'rep_1'=2,'rep_2'=2,'stripe_0'=4,'stripe_1'=4] {'rep_1'}, use_global_device_ids=true, to_apply=%region_4.5 | all-reduce | flops 1 | bytes 8 | tf_op jit(solution)/shard_map/psum | solution.py:24
  211.6 9.8 %psum.107 = f32[]{:T(128)} all-reduce(f32[]{:T(128)} %psum.106), channel_id=1, replica_groups=mesh['rep_0'=4,'rep_1'=2,'rep_2'=2,'stripe_0'=4,'stripe_1'=4] {'rep_2'}, use_global_device_ids=true, to_apply=%region_5.6 | all-reduce | flops 1 | bytes 8 | tf_op jit(solution)/shard_map/psum | solution.py:24
  221.4 7.5 %psum.108 = f32[]{:T(128)} all-reduce(f32[]{:T(128)} %psum.107), channel_id=1, replica_groups=mesh['rep_0'=4,'rep_1'=2,'rep_2'=2,'stripe_0'=4,'stripe_1'=4] {'stripe_0'}, use_global_device_ids=true, to_apply=%region_6.7 | all-reduce | flops 1 | bytes 8 | tf_op jit(solution)/shard_map/psum | solution.py:24
  228.9 10.8 %psum.109 = f32[]{:T(128)} all-reduce(f32[]{:T(128)} %psum.108), channel_id=1, replica_groups=mesh['rep_0'=4,'rep_1'=2,'rep_2'=2,'stripe_0'=4,'stripe_1'=4] {'stripe_1'}, use_global_device_ids=true, to_apply=%region_7.8 | all-reduce | flops 1 | bytes 8 | tf_op jit(solution)/shard_map/psum | solution.py:24
  242.0 2.0 fusion.12
  244.0 1.8 fusion.46
  245.8 1.9 fusion.4
  247.8 3.1 fusion.9
  250.9 1.8 fusion.47
  254.2 20.9 %collective-permute-done.1 = f32[512,512]{1,0:T(8,128)S(1)} collective-permute-done((f32[512,512]{1,0:T(8,128)S(1)}, f32[512,512]{1,0:T(8,128)S(1)}, u32[]{:S(2)}, u32[]{:S(2)}) %collective-permute-start.1) | collective-permute-done | bytes 1048608 | tf_op jit(solution)/shard_map/ppermute | solution.py:19
  275.0 2.7 fusion.15
  277.8 1.8 multiply_reduce_fusion.1
  279.5 6.6 %all-reduce.2 = (f32[]{:T(128)}, f32[]{:T(128)}) all-reduce(f32[]{:T(128)} %multiply_reduce_fusion.2, f32[]{:T(128)} %get-tuple-element.14), channel_id=1, replica_groups=mesh['rep_0'=4,'rep_1'=2,'rep_2'=2,'stripe_0'=4,'stripe_1'=4] {'rep_0'}, use_global_device_ids=true, to_apply=%region_10.11 | all-reduce | flops 2 | bytes 16 | tf_op jit(solution)/shard_map/psum | solution.py:24
  286.1 8.4 %all-reduce.4 = (f32[]{:T(128)}, f32[]{:T(128)}) all-reduce(f32[]{:T(128)} %get-tuple-element.6, f32[]{:T(128)} %get-tuple-element.7), channel_id=1, replica_groups=mesh['rep_0'=4,'rep_1'=2,'rep_2'=2,'stripe_0'=4,'stripe_1'=4] {'rep_1'}, use_global_device_ids=true, to_apply=%region_11.12 | all-reduce | flops 2 | bytes 16 | tf_op jit(solution)/shard_map/psum | solution.py:24
  294.5 10.6 %all-reduce.3 = (f32[]{:T(128)}, f32[]{:T(128)}) all-reduce(f32[]{:T(128)} %get-tuple-element.10, f32[]{:T(128)} %get-tuple-element.11), channel_id=1, replica_groups=mesh['rep_0'=4,'rep_1'=2,'rep_2'=2,'stripe_0'=4,'stripe_1'=4] {'rep_2'}, use_global_device_ids=true, to_apply=%region_12.13 | all-reduce | flops 2 | bytes 16 | tf_op jit(solution)/shard_map/psum | solution.py:24
  305.1 6.8 %all-reduce.1 = (f32[]{:T(128)}, f32[]{:T(128)}) all-reduce(f32[]{:T(128)} %get-tuple-element.8, f32[]{:T(128)} %get-tuple-element.9), channel_id=1, replica_groups=mesh['rep_0'=4,'rep_1'=2,'rep_2'=2,'stripe_0'=4,'stripe_1'=4] {'stripe_0'}, use_global_device_ids=true, to_apply=%region_13.14 | all-reduce | flops 2 | bytes 16 | tf_op jit(solution)/shard_map/psum | solution.py:24
  311.8 7.2 %all-reduce = (f32[]{:T(128)}, f32[]{:T(128)}) all-reduce(f32[]{:T(128)} %get-tuple-element.4, f32[]{:T(128)} %get-tuple-element.5), channel_id=1, replica_groups=mesh['rep_0'=4,'rep_1'=2,'rep_2'=2,'stripe_0'=4,'stripe_1'=4] {'stripe_1'}, use_global_device_ids=true, to_apply=%region_14.15 | all-reduce | flops 2 | bytes 16 | tf_op jit(solution)/shard_map/psum | solution.py:24
  321.4 107.2 %all-gather.3.cloned.1.call-done = f32[4096,512]{1,0:T(8,128)} async-done(((f32[256,512]{1,0:T(8,128)}), f32[4096,512]{1,0:T(8,128)}) %all-gather.3.cloned.1.call-update) | async-done | bytes 8388624 | tf_op jit(solution)/shard_map/all_gather | solution.py:98
  428.6 7.7 %gather_fusion.2 = f32[16,256,512]{2,1,0:T(8,128)} fusion(f32[16,256,512]{2,1,0:T(8,128)} %bitcast.41, s32[1024]{0:T(1024)S(1)} %pad_clamp_fusion), kind=kCustom, calls=%fused_computation.2 | custom fusion | bytes 16777280 | tf_op jit(solution)/shard_map/jit(_take)/gather | solution.py:104
  436.3 6.0 %bitcast_select_fusion = f32[4096,512]{1,0:T(8,128)} fusion(f32[16,256,512]{2,1,0:T(8,128)} %gather_fusion.2, pred[4096]{0:T(1024)(128)(4,1)S(1)} %broadcast_in_dim.40), kind=kLoop, calls=%fused_computation.3 | loop fusion | flops 2097152 | bytes 16781312 | tf_op jit(solution)/shard_map/jit(_take)/select_n | solution.py:104
  (32 shorter events, 4.8 us)
Async XLA Ops:
  7.2 11.4 %copy-start = (bf16[256,512]{1,0:T(8,128)(2,1)S(1)}, bf16[256,512]{1,0:T(8,128)(2,1)}, u32[]{:S(2)}) copy-start(bf16[256,512]{1,0:T(8,128)(2,1)} %param.5) | copy-start | bytes 786436
  7.2 169.2 %reduce-scatter.2.cloned.1.call-start = ((), (), s32[]{:S(2)}) async-start(), calls=%async_computation.1 | async-start | bytes 8912896 | tf_op jit(solution)/shard_map/reduce_scatter | solution.py:64
  34.2 394.5 %all-gather.3.cloned.1.call-start = ((), (), s32[]{:S(2)}) async-start(), calls=%async_computation.2 | async-start | bytes 8912896 | tf_op jit(solution)/shard_map/all_gather | solution.py:98
  176.3 12.9 %collective-permute-start = (f32[256,512]{0,1:T(8,128)}, f32[256,512]{0,1:T(8,128)S(1)}, u32[]{:S(2)}, u32[]{:S(2)}) collective-permute-start(f32[256,512]{0,1:T(8,128)} %reduce-scatter.2.cloned.1.call-done), channel_id=1, source_target_pairs={{0,128},{16,144},{32,160},{48,176},{64,192},{80,208},{96,224},{112... | collective-permute-start | bytes 1572872 | tf_op jit(solution)/shard_map/ppermute | solution.py:19
  189.3 1.6 copy-start.3
  196.8 45.2 %copy-start.1 = (f32[512,512]{1,0:T(8,128)}, f32[512,512]{1,0:T(8,128)S(1)}, u32[]{:S(2)}) copy-start(f32[512,512]{1,0:T(8,128)S(1)} %get-tuple-element.13) | copy-start | bytes 3145732
  244.0 1.9 copy-start.2
  252.8 22.3 %collective-permute-start.1 = (f32[512,512]{1,0:T(8,128)S(1)}, f32[512,512]{1,0:T(8,128)S(1)}, u32[]{:S(2)}, u32[]{:S(2)}) collective-permute-start(f32[512,512]{1,0:T(8,128)S(1)} %fusion.47), channel_id=1, source_target_pairs={{0,128},{16,144},{32,160},{48,176},{64,192},{80,208},{96,224},{112... | collective-permute-start | bytes 3145736 | tf_op jit(solution)/shard_map/ppermute | solution.py:19
Sparse Core Ops, SparseCore 0:
  34.3 142.0 reduce-scatter.1
  321.3 107.2 all-gather.2
where the time goes:
time: 450 us; the launch traced here: 449 us
  waiting for transfers between devices  282 us (63%)
  blocking collectives  82.5 us (18%)
  local copies, waits for them, and re-layouts  27.6 us (6%)
  matrix products  27.4 us (6%)
  between operations  16.8 us (4%)
  other arithmetic  10.9 us (2%)
    reduce_scatter x1, waiting for transfers between devices, per_device(): lax.psum_scatter(slot_terms(activations, out_grads, blocks_of, pair_count...  142 us
    all_gather x1, waiting for transfers between devices, per_device(): gathered = lax.all_gather(scaled[None], REP, axis=0, tiled=True)  107 us
    psum x10, blocking collectives, by_axis(): shard = lax.psum(shard, axis)  82.5 us
    ppermute x2, waiting for transfers between devices, partner(): lax.ppermute(shard, axis, [(i, i ^ 1 << stride) for i in range(lax.axis_s...  32.6 us
  transfers between devices with their start and end apart: 4, of which 4 were waited for; matrix products, arithmetic and copies ran while one was open for 0% of the time, Pallas kernels for 0%

commit v1 on v0

--- a/solution.py
+++ b/solution.py
@@ -95,7 +95,9 @@
         by_axis(jnp.sum(precond_half * precond_half), REP_STRIPE),
     )
     scaled = precond_half * jnp.sqrt(grad_sq / (prec_sq + epsilon))
-    gathered = lax.all_gather(scaled[None], REP, axis=0, tiled=True)
+    own = scaled[None]
+    repeated = jnp.stack([own] * lax.axis_size(REP))
+    gathered = jnp.concatenate(lax.all_to_all(repeated, REP, 0, 0), axis=0)
     pair_ids = jnp.arange(pair_count, dtype=jnp.int32)
     inverse = jnp.sum(
         pair_ids[:, None] * (blocks_of[:, None] == pair_ids[None, :]).astype(jnp.int32), axis=0

time: 450 us -> 543 us (1.21)
  waiting for transfers between devices: 282 us -> 362 us
  starting transfers between devices: 1.94 us -> 10.5 us
    all_to_all x0 -> x1, waiting for transfers between devices: none -> 187 us  [per_device(): gathered = jnp.concatenate(lax.all_to_all(repeated, REP, 0, 0), axis=0)]
    all_gather x1 -> x0, waiting for transfers between devices: 107 us -> none  [per_device(): gathered = lax.all_gather(scaled[None], REP, axis=0, tiled=True)]
    all_to_all x0 -> x1, starting transfers between devices: none -> 8.63 us  [per_device(): gathered = jnp.concatenate(lax.all_to_all(repeated, REP, 0, 0), axis=0)]
where the time goes in v1:
time: 543 us; the launch traced here: 542 us
  waiting for transfers between devices  362 us (67%)
  blocking collectives  82.5 us (15%)
  local copies, waits for them, and re-layouts  32.1 us (6%)
  matrix products  28.6 us (5%)
  between operations  16.8 us (3%)
  starting transfers between devices  10.5 us (2%)
  other arithmetic  10.1 us (2%)
    all_to_all x1, waiting for transfers between devices, per_device(): gathered = jnp.concatenate(lax.all_to_all(repeated, REP, 0, 0), axis=0)  187 us
    reduce_scatter x1, waiting for transfers between devices, per_device(): lax.psum_scatter(slot_terms(activations, out_grads, blocks_of, pair_count...  142 us
    psum x10, blocking collectives, by_axis(): shard = lax.psum(shard, axis)  82.5 us
    ppermute x2, waiting for transfers between devices, partner(): lax.ppermute(shard, axis, [(i, i ^ 1 << stride) for i in range(lax.axis_s...  32.6 us
  transfers between devices with their start and end apart: 4, of which 4 were waited for; matrix products, arithmetic and copies ran while one was open for 0% of the time, Pallas kernels for 0%

profile of v1, /device:TPU:1, one launch (start us, length us, event | category | flops | bytes accessed | tf_op | source)
XLA Modules:
  0.0 542.4 jit_solution(7513989068470181018)
XLA Ops:
  9.6 4.1 copy.26
  13.7 2.8 copy.27
  16.5 2.0 gather_fusion.1
  18.5 6.7 %fusion = f32[16,256,512]{2,1,0:T(8,128)} fusion(bf16[16,256,256]{2,1,0:T(8,128)(2,1)} %gather_fusion.1, pred[16]{0:T(512)(128)(4,1)S(1)} %get-tuple-element.16, bf16[256,512]{1,0:T(8,128)(2,1)S(1)} %copy-done), kind=kOutput, calls=%fused_computation.4 | convolution fusion | flops 1074790400 | bytes 10747920 | tf_op jit(solution)/shard_map/tkp,tc->kpc/dot_general | solution.py:52
  25.2 8.9 %copy.29 = f32[4096,512]{0,1:T(8,128)} copy(f32[4096,512]{1,0:T(8,128)} %bitcast.40) | data formatting | bytes 16777216 | tf_op jit(solution)/shard_map/reshape | solution.py:53
  34.2 142.2 %reduce-scatter.2.cloned.1.call-done = f32[256,512]{0,1:T(8,128)} async-done(((f32[4096,512]{0,1:T(8,128)}), f32[256,512]{0,1:T(8,128)}) %reduce-scatter.2.cloned.1.call-update) | async-done | bytes 524304 | tf_op jit(solution)/shard_map/reduce_scatter | solution.py:64
  177.5 11.8 %collective-permute-done = f32[256,512]{0,1:T(8,128)S(1)} collective-permute-done((f32[256,512]{0,1:T(8,128)}, f32[256,512]{0,1:T(8,128)S(1)}, u32[]{:S(2)}, u32[]{:S(2)}) %collective-permute-start) | collective-permute-done | bytes 524320 | tf_op jit(solution)/shard_map/ppermute | solution.py:19
  189.3 1.6 maximum_select_fusion
  191.2 5.6 %select_reduce_fusion = (f32[]{:T(128)}, f32[512,512]{1,0:T(8,128)S(1)}) fusion(f32[512,512]{1,0:T(8,128)S(1)} %copy.31, pred[]{:T(512)S(6)} %lt.75, f32[256,512]{0,1:T(8,128)} %reduce-scatter.2.cloned.1.call-done, f32[256,512]{0,1:T(8,128)} %copy-done.3, f32[1,1,512,512]{3,2,1,0:T(8,128)} %param.6), kind=kOutput, calls=%fused_computation.22 | convolution fusion | flops 1612972032 | bytes 4194309 | tf_op jit(solution)/shard_map/dot_general | solution.py:79
  196.7 6.6 %psum.105 = f32[]{:T(128)} all-reduce(f32[]{:T(128)} %get-tuple-element.12), channel_id=1, replica_groups=mesh['rep_0'=4,'rep_1'=2,'rep_2'=2,'stripe_0'=4,'stripe_1'=4] {'rep_0'}, use_global_device_ids=true, to_apply=%region_3.4 | all-reduce | flops 1 | bytes 8 | tf_op jit(solution)/shard_map/psum | solution.py:24
  203.3 8.3 %psum.106 = f32[]{:T(128)} all-reduce(f32[]{:T(128)} %psum.105), channel_id=1, replica_groups=mesh['rep_0'=4,'rep_1'=2,'rep_2'=2,'stripe_0'=4,'stripe_1'=4] {'rep_1'}, use_global_device_ids=true, to_apply=%region_4.5 | all-reduce | flops 1 | bytes 8 | tf_op jit(solution)/shard_map/psum | solution.py:24
  211.6 9.8 %psum.107 = f32[]{:T(128)} all-reduce(f32[]{:T(128)} %psum.106), channel_id=1, replica_groups=mesh['rep_0'=4,'rep_1'=2,'rep_2'=2,'stripe_0'=4,'stripe_1'=4] {'rep_2'}, use_global_device_ids=true, to_apply=%region_5.6 | all-reduce | flops 1 | bytes 8 | tf_op jit(solution)/shard_map/psum | solution.py:24
  221.4 7.5 %psum.108 = f32[]{:T(128)} all-reduce(f32[]{:T(128)} %psum.107), channel_id=1, replica_groups=mesh['rep_0'=4,'rep_1'=2,'rep_2'=2,'stripe_0'=4,'stripe_1'=4] {'stripe_0'}, use_global_device_ids=true, to_apply=%region_6.7 | all-reduce | flops 1 | bytes 8 | tf_op jit(solution)/shard_map/psum | solution.py:24
  228.9 10.8 %psum.109 = f32[]{:T(128)} all-reduce(f32[]{:T(128)} %psum.108), channel_id=1, replica_groups=mesh['rep_0'=4,'rep_1'=2,'rep_2'=2,'stripe_0'=4,'stripe_1'=4] {'stripe_1'}, use_global_device_ids=true, to_apply=%region_7.8 | all-reduce | flops 1 | bytes 8 | tf_op jit(solution)/shard_map/psum | solution.py:24
  241.9 2.0 fusion.12
  244.0 1.8 fusion.46
  245.8 3.1 fusion.4
  249.0 3.1 fusion.9
  252.1 1.8 fusion.47
  255.4 20.9 %collective-permute-done.1 = f32[512,512]{1,0:T(8,128)S(1)} collective-permute-done((f32[512,512]{1,0:T(8,128)S(1)}, f32[512,512]{1,0:T(8,128)S(1)}, u32[]{:S(2)}, u32[]{:S(2)}) %collective-permute-start.1) | collective-permute-done | bytes 1048608 | tf_op jit(solution)/shard_map/ppermute | solution.py:19
  276.2 2.7 fusion.15
  278.9 1.8 multiply_reduce_fusion.1
  280.7 6.6 %all-reduce.2 = (f32[]{:T(128)}, f32[]{:T(128)}) all-reduce(f32[]{:T(128)} %multiply_reduce_fusion.2, f32[]{:T(128)} %get-tuple-element.14), channel_id=1, replica_groups=mesh['rep_0'=4,'rep_1'=2,'rep_2'=2,'stripe_0'=4,'stripe_1'=4] {'rep_0'}, use_global_device_ids=true, to_apply=%region_10.11 | all-reduce | flops 2 | bytes 16 | tf_op jit(solution)/shard_map/psum | solution.py:24
  287.3 8.4 %all-reduce.4 = (f32[]{:T(128)}, f32[]{:T(128)}) all-reduce(f32[]{:T(128)} %get-tuple-element.6, f32[]{:T(128)} %get-tuple-element.7), channel_id=1, replica_groups=mesh['rep_0'=4,'rep_1'=2,'rep_2'=2,'stripe_0'=4,'stripe_1'=4] {'rep_1'}, use_global_device_ids=true, to_apply=%region_11.12 | all-reduce | flops 2 | bytes 16 | tf_op jit(solution)/shard_map/psum | solution.py:24
  295.7 10.6 %all-reduce.3 = (f32[]{:T(128)}, f32[]{:T(128)}) all-reduce(f32[]{:T(128)} %get-tuple-element.10, f32[]{:T(128)} %get-tuple-element.11), channel_id=1, replica_groups=mesh['rep_0'=4,'rep_1'=2,'rep_2'=2,'stripe_0'=4,'stripe_1'=4] {'rep_2'}, use_global_device_ids=true, to_apply=%region_12.13 | all-reduce | flops 2 | bytes 16 | tf_op jit(solution)/shard_map/psum | solution.py:24
  306.3 6.8 %all-reduce.1 = (f32[]{:T(128)}, f32[]{:T(128)}) all-reduce(f32[]{:T(128)} %get-tuple-element.8, f32[]{:T(128)} %get-tuple-element.9), channel_id=1, replica_groups=mesh['rep_0'=4,'rep_1'=2,'rep_2'=2,'stripe_0'=4,'stripe_1'=4] {'stripe_0'}, use_global_device_ids=true, to_apply=%region_13.14 | all-reduce | flops 2 | bytes 16 | tf_op jit(solution)/shard_map/psum | solution.py:24
  313.0 7.2 %all-reduce = (f32[]{:T(128)}, f32[]{:T(128)}) all-reduce(f32[]{:T(128)} %get-tuple-element.4, f32[]{:T(128)} %get-tuple-element.5), channel_id=1, replica_groups=mesh['rep_0'=4,'rep_1'=2,'rep_2'=2,'stripe_0'=4,'stripe_1'=4] {'stripe_1'}, use_global_device_ids=true, to_apply=%region_14.15 | all-reduce | flops 2 | bytes 16 | tf_op jit(solution)/shard_map/psum | solution.py:24
  321.6 4.5 stack.12
  326.1 8.6 %all-to-all-start = ((f32[16,1,256,512]{3,2,1,0:T(8,128)}), f32[16,1,256,512]{3,2,1,0:T(8,128)}, u32[]{:S(2)}, u32[]{:S(2)}) async-start(f32[16,1,256,512]{3,2,1,0:T(8,128)} %stack.12), calls=%async_computation.1 | async-start | bytes 16777216 | tf_op jit(solution)/shard_map/all_to_all | solution.py:100
  334.9 187.0 %all-to-all-done = f32[16,1,256,512]{3,2,1,0:T(8,128)} async-done(((f32[16,1,256,512]{3,2,1,0:T(8,128)}), f32[16,1,256,512]{3,2,1,0:T(8,128)}, u32[]{:S(2)}, u32[]{:S(2)}) %all-to-all-start) | async-done | bytes 8388640 | tf_op jit(solution)/shard_map/all_to_all | solution.py:100
  521.9 7.7 %gather_fusion.2 = f32[16,256,512]{2,1,0:T(8,128)} fusion(f32[16,256,512]{2,1,0:T(8,128)} %bitcast.11, s32[1024]{0:T(1024)S(1)} %pad_clamp_fusion), kind=kCustom, calls=%fused_computation.2 | custom fusion | bytes 16777280 | tf_op jit(solution)/shard_map/jit(_take)/gather | solution.py:106
  529.6 6.0 %bitcast_select_fusion = f32[4096,512]{1,0:T(8,128)} fusion(f32[16,256,512]{2,1,0:T(8,128)} %gather_fusion.2, pred[4096]{0:T(1024)(128)(4,1)S(1)} %broadcast_in_dim.37), kind=kLoop, calls=%fused_computation.3 | loop fusion | flops 2097152 | bytes 16781312 | tf_op jit(solution)/shard_map/jit(_take)/select_n | solution.py:106
  (32 shorter events, 6.5 us)
Async XLA Ops:
  7.2 11.4 %copy-start = (bf16[256,512]{1,0:T(8,128)(2,1)S(1)}, bf16[256,512]{1,0:T(8,128)(2,1)}, u32[]{:S(2)}) copy-start(bf16[256,512]{1,0:T(8,128)(2,1)} %param.5) | copy-start | bytes 786436
  7.2 169.2 %reduce-scatter.2.cloned.1.call-start = ((), (), s32[]{:S(2)}) async-start(), calls=%async_computation.2 | async-start | bytes 8912896 | tf_op jit(solution)/shard_map/reduce_scatter | solution.py:64
  176.3 12.9 %collective-permute-start = (f32[256,512]{0,1:T(8,128)}, f32[256,512]{0,1:T(8,128)S(1)}, u32[]{:S(2)}, u32[]{:S(2)}) collective-permute-start(f32[256,512]{0,1:T(8,128)} %reduce-scatter.2.cloned.1.call-done), channel_id=1, source_target_pairs={{0,128},{16,144},{32,160},{48,176},{64,192},{80,208},{96,224},{112... | collective-permute-start | bytes 1572872 | tf_op jit(solution)/shard_map/ppermute | solution.py:19
  189.3 1.6 copy-start.3
  196.7 45.2 %copy-start.2 = (f32[512,512]{1,0:T(8,128)}, f32[512,512]{1,0:T(8,128)S(1)}, u32[]{:S(2)}) copy-start(f32[512,512]{1,0:T(8,128)S(1)} %get-tuple-element.13) | copy-start | bytes 3145732
  254.0 22.3 %collective-permute-start.1 = (f32[512,512]{1,0:T(8,128)S(1)}, f32[512,512]{1,0:T(8,128)S(1)}, u32[]{:S(2)}, u32[]{:S(2)}) collective-permute-start(f32[512,512]{1,0:T(8,128)S(1)} %fusion.47), channel_id=1, source_target_pairs={{0,128},{16,144},{32,160},{48,176},{64,192},{80,208},{96,224},{112... | collective-permute-start | bytes 3145736 | tf_op jit(solution)/shard_map/ppermute | solution.py:19
  326.1 195.8 %all-to-all-start = ((f32[16,1,256,512]{3,2,1,0:T(8,128)}), f32[16,1,256,512]{3,2,1,0:T(8,128)}, u32[]{:S(2)}, u32[]{:S(2)}) async-start(f32[16,1,256,512]{3,2,1,0:T(8,128)} %stack.12), calls=%async_computation.1 | async-start | bytes 16777216 | tf_op jit(solution)/shard_map/all_to_all | solution.py:100
  521.9 13.7 %copy-start.1 = (bf16[256,512]{1,0:T(8,128)(2,1)S(1)}, bf16[256,512]{1,0:T(8,128)(2,1)}, u32[]{:S(2)}) copy-start(bf16[256,512]{1,0:T(8,128)(2,1)} %param.5) | copy-start | bytes 786436
Sparse Core Ops, SparseCore 0:
  34.3 142.0 reduce-scatter.1
